TPU v7x, 32 devices: a whole 2x2x4 slice. The times are simulated.
32 devices in a mesh: row: 4 (over y, core), col: 8 (over z, x).
Axes of the slice: x: 2, y: 2, z: 4, core: 2. Of those that a mesh axis runs over, the one named last changes fastest.
Arguments:
- tokens: bfloat16 [64, 16384], P('row', 'col'), may hold values from -6 to 6
- gate_weight: bfloat16 [16384, 26624], P('col', 'row'), may hold values from -0.046875 to 0.046875
- up_weight: bfloat16 [16384, 26624], P('col', 'row'), may hold values from -0.046875 to 0.046875
Outputs:
- hidden: bfloat16 [64, 26624], P(None, 'row')
All inputs are finite; a program needn't handle non-finite values.
Results may differ from a plain program's by a relative error of at most 0.001.
Values may be sent and summed in bfloat16 or wider, within the bound.
A program may use at most 128 MiB of HBM per device.

v0:
```python
import functools

import jax
import jax.numpy as jnp
from jax import lax
from jax.experimental import pallas as pl
from jax.experimental.pallas import tpu as pltpu
from jax.sharding import PartitionSpec as P

MESH = pl.DeviceIdType.MESH

BUFFERS = 4
LAG = 3
WIDEST = 512
GATHER_REVERSED = True


def digits_of(n):
    bits = n.bit_length() - 1
    out = [(1, 2)]
    weight = 2
    if SPLIT_Z:
        for _ in range(bits - 1):
            out.append((weight, 2))
            weight *= 2
    elif bits > 1:
        out.append((2, n // 2))
    return out


SPLIT_Z = True


LANES = 128
SPAN, FLOOR = 175.0, -87.0


def across(tile, width):
    return jnp.concatenate([tile] * (width // LANES), axis=1)


def encode(x, inverse):
    size = jnp.exp(jnp.abs(x) * across(inverse * SPAN, x.shape[1]) + FLOOR)
    return jnp.where(x < 0, -size, size).astype(jnp.bfloat16)


def decode(y, peak):
    y = y.astype(jnp.float32)
    size = (jnp.log(jnp.abs(y)) - FLOOR) * across(peak * (1.0 / SPAN), y.shape[1])
    return jnp.where(y < 0, -size, size)


def kernel(n_row, n_col, chunks, width, tok_hbm, gate_hbm, up_hbm, out_hbm, *scratch):
    digits = digits_of(n_col)
    stages = len(digits)
    xg, wbuf, acc = scratch[0:3]
    held = scratch[3 : 3 + stages - 1]
    scratch = scratch[2 + stages :]
    sends, recvs, (gath, ) = scratch[:stages], scratch[stages : 2 * stages], scratch[2 * stages : 2 * stages + 1]
    tok_sem, tok_send, tok_recv, w_sem, out_sem = scratch[2 * stages + 1 : 2 * stages + 6]
    rs_send = scratch[2 * stages + 6 : 3 * stages + 6]
    rs_recv = scratch[3 * stages + 6 : 4 * stages + 6]
    ag_send = scratch[4 * stages + 6 : 5 * stages + 6]
    ag_recv = scratch[5 * stages + 6 : 6 * stages + 6]

    row, col = lax.axis_index("row"), lax.axis_index("col")
    mine = [(col // weight) % radix for weight, radix in digits]

    def peer(stage, offset):
        weight, radix = digits[stage]
        return col + ((mine[stage] + offset) % radix - mine[stage]) * weight

    def weights(c, slot):
        cols = pl.ds(pl.multiple_of(c * width, width), width)
        return [
            pltpu.make_async_copy(hbm.at[:, cols], wbuf.at[slot, k], w_sem.at[slot, k])
            for k, hbm in enumerate((gate_hbm, up_hbm))
        ]

    own = pltpu.make_async_copy(tok_hbm, xg.at[row], tok_sem)
    own.start()
    for c in range(min(BUFFERS, chunks)):
        for copy in weights(c, c):
            copy.start()

    barrier = pltpu.get_barrier_semaphore()
    greeted = 0
    for o in range(1, n_row):
        pl.semaphore_signal(barrier, inc=1, device_id=((row + o) % n_row, col), device_id_type=MESH)
        greeted += 1
    for i, (_, radix) in enumerate(digits):
        for o in range(1, radix):
            pl.semaphore_signal(barrier, inc=1, device_id=(row, peer(i, o)), device_id_type=MESH)
            greeted += 1
    pl.semaphore_wait(barrier, greeted)
    own.wait()

    def token_copy(o, place):
        return pltpu.make_async_remote_copy(
            src_ref=xg.at[place], dst_ref=xg.at[place], send_sem=tok_send.at[o - 1], recv_sem=tok_recv.at[o - 1],
            device_id=((row + o) % n_row, col), device_id_type=MESH)

    for o in range(1, n_row):
        token_copy(o, row).start()
    for o in range(1, n_row):
        token_copy(o, (row + n_row - o) % n_row).wait_recv()
    for o in range(1, n_row):
        token_copy(o, row).wait_send()

    def rs_copy(i, o, c):
        return pltpu.make_async_remote_copy(
            src_ref=sends[i].at[c, o - 1], dst_ref=recvs[i].at[c, o - 1],
            send_sem=rs_send[i].at[o - 1, c], recv_sem=rs_recv[i].at[o - 1, c],
            device_id=(row, peer(i, o)), device_id_type=MESH)

    def send_parts(i, source, c):
        sub = source.shape[1] // digits[i][1]
        for o in range(1, digits[i][1]):
            to = (mine[i] + o) % digits[i][1]
            for k in range(2):
                parts = [source[c, to * sub + g, k] for g in range(sub)]
                peak = functools.reduce(jnp.maximum, [
                    jnp.abs(part[:, at : at + LANES]) for part in parts for at in range(0, width, LANES)])
                peak = jnp.maximum(peak * 1.01, 1e-37).astype(jnp.bfloat16)
                sends[i][c, o - 1, k, :, sub * width :] = peak
                inverse = 1.0 / peak.astype(jnp.float32)
                for g, part in enumerate(parts):
                    sends[i][c, o - 1, k, :, g * width : (g + 1) * width] = encode(part, inverse)
            rs_copy(i, o, c).start()

    def summed(i, source, c, sink):
        sub = source.shape[1] // digits[i][1]
        for o in range(1, digits[i][1]):
            rs_copy(i, o, c).wait_recv()
        for k in range(2):
            peaks = [recvs[i][c, o, k, :, sub * width :].astype(jnp.float32) for o in range(digits[i][1] - 1)]
            for g in range(sub):
                total = source[c, mine[i] * sub + g, k]
                for o, peak in enumerate(peaks):
                    total = total + decode(recvs[i][c, o, k, :, g * width : (g + 1) * width], peak)
                sink(g, k, total)

    order = list(range(stages))[::-1] if GATHER_REVERSED else list(range(stages))

    def gathered_place(a, c, shift):
        index = [c]
        for i in range(stages):
            if i in order[:a]:
                index.append(slice(None))
            elif i == order[a]:
                index.append((mine[i] + digits[i][1] + shift) % digits[i][1])
            else:
                index.append(mine[i])
        return gath.at[tuple(index)]

    def ag_copy(a, o, c, shift):
        ref = gathered_place(a, c, shift)
        return pltpu.make_async_remote_copy(
            src_ref=ref, dst_ref=ref, send_sem=ag_send[a].at[o - 1, c], recv_sem=ag_recv[a].at[o - 1, c],
            device_id=(row, peer(order[a], o)), device_id_type=MESH)

    def ag_start(a, c):
        for o in range(1, digits[order[a]][1]):
            ag_copy(a, o, c, 0).start()

    def ag_wait(a, c):
        for o in range(1, digits[order[a]][1]):
            ag_copy(a, o, c, -o).wait_recv()

    def out_copy(c):
        cols = pl.ds(pl.multiple_of(c * width, width), width)
        return pltpu.make_async_copy(gath.at[c], out_hbm.at[(slice(None),) * (stages + 1) + (cols,)], out_sem.at[c])

    def multiply(c):
        slot = c % BUFFERS
        for k, copy in enumerate(weights(c, slot)):
            copy.wait()
            x = xg[...].reshape(-1, xg.shape[-1])
            part = jnp.dot(x, wbuf[slot, k], preferred_element_type=jnp.float32)
            acc[c, :, k] = part.reshape(n_col, -1, width)
        send_parts(0, acc, c)

        @pl.when(c + BUFFERS < chunks)
        def _():
            for copy in weights(c + BUFFERS, slot):
                copy.start()

    def reduce_step(i, c):
        source = acc if i == 0 else held[i - 1]
        if i < stages - 1:
            def keep(g, k, total):
                held[i][c, g, k] = total

            summed(i, source, c, keep)
            send_parts(i + 1, held[i], c)
        else:
            sums = []
            summed(i, source, c, lambda g, k, total: sums.append(total))
            gate, up = sums
            gath[(c, *mine)] = (gate / (1.0 + jnp.exp(-gate)) * up).astype(jnp.bfloat16)
            ag_start(0, c)

    def gather_step(a, c):
        ag_wait(a, c)
        if a < stages - 1:
            ag_start(a + 1, c)
        else:
            out_copy(c).start()

    steps = [multiply]
    steps += [functools.partial(reduce_step, i) for i in range(stages)]
    steps += [functools.partial(gather_step, a) for a in range(stages)]

    def turn(t, carry):
        for s, step in enumerate(steps):
            c = t - s * LAG

            @pl.when(jnp.logical_and(c >= 0, c < chunks))
            def _(c=c, step=step):
                step(c)

        return carry

    lax.fori_loop(0, chunks + (len(steps) - 1) * LAG, turn, 0)

    def drain(c, carry):
        for i in range(stages):
            for o in range(1, digits[i][1]):
                rs_copy(i, o, c).wait_send()
        for a in range(stages):
            for o in range(1, digits[order[a]][1]):
                ag_copy(a, o, c, 0).wait_send()
        out_copy(c).wait()
        return carry

    lax.fori_loop(0, chunks, drain, 0)


def solution(mesh):
    n_row, n_col = mesh.shape["row"], mesh.shape["col"]

    def local(tokens, gate_weight, up_weight):
        own_tokens, depth = tokens.shape
        columns = gate_weight.shape[1]
        each = own_tokens * n_row // n_col
        width = max(w for w in range(128, WIDEST + 1, 128) if columns % w == 0)
        chunks = columns // width
        digits = digits_of(n_col)
        radices = tuple(radix for _, radix in digits)
        subs, count = [], n_col
        for radix in radices:
            count //= radix
            subs.append(count)
        parts = [(chunks, radix - 1, 2, each, sub * width + LANES) for radix, sub in zip(radices, subs)]
        scratch = [
            pltpu.VMEM((n_row, own_tokens, depth), jnp.bfloat16),
            pltpu.VMEM((BUFFERS, 2, depth, width), jnp.bfloat16),
            pltpu.VMEM((chunks, n_col, 2, each, width), jnp.float32),
        ]
        scratch += [pltpu.VMEM((chunks, sub, 2, each, width), jnp.float32) for sub in subs[:-1]]
        scratch += [pltpu.VMEM(shape, jnp.bfloat16) for shape in parts]
        scratch += [pltpu.VMEM(shape, jnp.bfloat16) for shape in parts]
        scratch += [pltpu.VMEM((chunks, *radices, each, width), jnp.bfloat16)]
        dma = pltpu.SemaphoreType.DMA
        scratch += [dma, dma((n_row - 1,)), dma((n_row - 1,)), dma((BUFFERS, 2)), dma((chunks,))]
        for _ in range(2):
            scratch += [dma((radix - 1, chunks)) for radix in radices]
        ordered = radices[::-1] if GATHER_REVERSED else radices
        for _ in range(2):
            scratch += [dma((radix - 1, chunks)) for radix in ordered]
        out = pl.pallas_call(
            functools.partial(kernel, n_row, n_col, chunks, width),
            out_shape=jax.ShapeDtypeStruct((*radices, each, columns), jnp.bfloat16),
            in_specs=[pl.BlockSpec(memory_space=pl.ANY)] * 3,
            out_specs=pl.BlockSpec(memory_space=pl.ANY),
            scratch_shapes=scratch,
            compiler_params=pltpu.CompilerParams(
                collective_id=0, has_side_effects=True, vmem_limit_bytes=60 * 2**20),
        )(tokens, gate_weight, up_weight)
        return out.reshape(n_col * each, columns)

    in_specs = (P("row", "col"), P("col", "row"), P("col", "row"))
    return jax.shard_map(local, mesh=mesh, in_specs=in_specs, out_specs=P(None, "row"), check_vma=False)
```

profile of v0, /device:TPU:0, one launch (start us, length us, event | category | flops | bytes accessed | tf_op | source)
XLA Modules:
  0.0 57.1 jit_solution(1674471306163616208)
XLA Ops:
  0.0 55.0 %shard_map.37 = bf16[2,2,2,8,6656]{4,3,2,1,0:T(8,128)(2,1)} custom-call(bf16[16,2048]{1,0:T(8,128)(2,1)} %tok_hbm.1, bf16[2048,6656]{1,0:T(8,128)(2,1)} %gate_hbm.1, bf16[2048,6656]{1,0:T(8,128)(2,1)} %up_hbm.1), custom_call_target="tpu_custom_call" | custom-call | tf_op jit(solution)/shard_map/pallas_call | solution.py:271
  55.0 2.1 %copy.5 = bf16[64,6656]{1,0:T(8,128)(2,1)} copy(bf16[64,6656]{1,0:T(8,128)(2,1)} %bitcast.1) | data formatting | bytes 1703936
where the time goes:
time: 57.3 us; the launch traced here: 57.1 us
  Pallas kernels  55 us (96%)
  local copies, waits for them, and re-layouts  2.11 us (4%)
    pallas_call x1, Pallas kernels, local(): pl.pallas_call(functools.partial(kernel, n_row, n_col, chunks, width), ou...  55 us
    unnamed x1, local copies, waits for them, and re-layouts  2.11 us

commit v1 on v0

v1 whole, which is shorter than its diff:
```python
import functools

import jax
import jax.numpy as jnp
from jax import lax
from jax.experimental import pallas as pl
from jax.experimental.pallas import tpu as pltpu
from jax.sharding import PartitionSpec as P

MESH = pl.DeviceIdType.MESH

BUFFERS = 8
LAGS = (0, 4, 7, 10)
GATHER_LAG = 3
FAR = 4
SWAP_EVERY = 4
SWAP_AT = (1, 3)
WIDEST = 512


def digits_of(n):
    bits = n.bit_length() - 1
    return [(2**i, 2) for i in range(bits)]


LANES = 128
SPAN, FLOOR = 175.0, -87.0


def across(tile, width):
    return jnp.concatenate([tile] * (width // LANES), axis=1)


def encode(x, inverse):
    size = jnp.exp(jnp.abs(x) * across(inverse * SPAN, x.shape[1]) + FLOOR)
    return jnp.where(x < 0, -size, size).astype(jnp.bfloat16)


def decode(y, peak):
    y = y.astype(jnp.float32)
    size = (jnp.log(jnp.abs(y)) - FLOOR) * across(peak * (1.0 / SPAN), y.shape[1])
    return jnp.where(y < 0, -size, size)


def kernel(n_row, n_col, chunks, width, tok_hbm, gate_hbm, up_hbm, out, *scratch):
    stages = len(digits_of(n_col))
    direct = min(FAR, chunks)
    xg, wbuf, acc = scratch[0:3]
    held = scratch[3 : 2 + stages]
    scratch = scratch[2 + stages :]
    sends, recvs = scratch[:stages], scratch[stages : 2 * stages]
    tok_sem, tok_send, tok_recv, w_sem, far_send, far_recv = scratch[2 * stages : 2 * stages + 6]
    scratch = scratch[2 * stages + 6 :]
    rs_send, ag_send = scratch[:2]
    rs_recv, ag_recv = scratch[2 : 2 + stages], scratch[2 + stages :]

    row, col = lax.axis_index("row"), lax.axis_index("col")

    def weights(c, slot):
        cols = pl.ds(pl.multiple_of(c * width, width), width)
        return [
            pltpu.make_async_copy(hbm.at[:, cols], wbuf.at[slot, k], w_sem.at[slot, k])
            for k, hbm in enumerate((gate_hbm, up_hbm))
        ]

    own = pltpu.make_async_copy(tok_hbm, xg.at[row], tok_sem)
    own.start()

    barrier = pltpu.get_barrier_semaphore()
    greeted = 0
    for o in range(1, n_row):
        pl.semaphore_signal(barrier, inc=1, device_id=((row + o) % n_row, col), device_id_type=MESH)
        greeted += 1
    for o in range(1, n_col):
        pl.semaphore_signal(barrier, inc=1, device_id=(row, (col + o) % n_col), device_id_type=MESH)
        greeted += 1
    own.wait()
    for c in range(min(BUFFERS, chunks)):
        for copy in weights(c, c):
            copy.start()
    pl.semaphore_wait(barrier, greeted)

    def token_copy(o, place):
        return pltpu.make_async_remote_copy(
            src_ref=xg.at[place], dst_ref=xg.at[place], send_sem=tok_send.at[o - 1], recv_sem=tok_recv.at[o - 1],
            device_id=((row + o) % n_row, col), device_id_type=MESH)

    for o in range(1, n_row):
        token_copy(o, row).start()
    for o in range(1, n_row):
        token_copy(o, (row + n_row - o) % n_row).wait_recv()
    for o in range(1, n_row):
        token_copy(o, row).wait_send()

    low = lax.broadcasted_iota(jnp.int32, (xg.shape[0] * xg.shape[1] // n_col, LANES), 1) < LANES // 2

    places = [(col // weight) % 2 for weight, _ in digits_of(n_col)]
    weighed = [weight for weight, _ in digits_of(n_col)]

    def ordered(values, c):
        turn = c % SWAP_EVERY
        swapped = jnp.where(row % 2 == 0, turn == SWAP_AT[0], turn == SWAP_AT[1])
        first, second, *rest = values
        return [jnp.where(swapped, second, first), jnp.where(swapped, first, second), *rest]

    def peer(i, c):
        return (row, col + ((1 - 2 * ordered(places, c)[i]) * ordered(weighed, c)[i]))

    def rs_copy(i, c):
        return pltpu.make_async_remote_copy(
            src_ref=sends[i].at[c], dst_ref=recvs[i].at[c], send_sem=rs_send.at[i], recv_sem=rs_recv[i].at[c],
            device_id=peer(i, c), device_id_type=MESH)

    def coded(i, source, c):
        sub = source.shape[1] // 2
        to = 1 - ordered(places, c)[i]
        peaks = []
        for k in range(2):
            parts = [source[c, to * sub + g, k] for g in range(sub)]
            peak = functools.reduce(jnp.maximum, [
                jnp.abs(part[:, at : at + LANES]) for part in parts for at in range(0, width, LANES)])
            peak = jnp.maximum(peak, pltpu.roll(peak, LANES // 2, 1))
            peak = jnp.maximum(peak * 1.01, 1e-37).astype(jnp.bfloat16).astype(jnp.float32)
            peaks.append(peak)
            inverse = 1.0 / peak
            for g, part in enumerate(parts):
                at = (k * sub + g) * width
                sends[i][c, :, at : at + width] = encode(part, inverse)
        sends[i][c, :, 2 * sub * width :] = jnp.where(low, *peaks).astype(jnp.bfloat16)

    def summed(i, source, c, sink):
        sub = source.shape[1] // 2
        both = recvs[i][c, :, 2 * sub * width :].astype(jnp.float32)
        swapped = pltpu.roll(both, LANES // 2, 1)
        peaks = jnp.where(low, both, swapped), jnp.where(low, swapped, both)
        at_home = ordered(places, c)[i] * sub
        for k in range(2):
            for g in range(sub):
                at = (k * sub + g) * width
                total = source[c, at_home + g, k] + decode(recvs[i][c, :, at : at + width], peaks[k])
                sink(g, k, total)

    def cols(c):
        return pl.ds(pl.multiple_of(c * width, width), width)

    def block(values, c):
        index = 0
        for value in ordered(values, c):
            index = index * 2 + value
        return index

    def ag_copy(a, c, back):
        own = block(places, c) // 2**a
        start = (own + (1 - 2 * (own % 2)) if back else own) * 2**a
        ref = out.at[pl.ds(start, 2**a), :, cols(c)]
        return pltpu.make_async_remote_copy(
            src_ref=ref, dst_ref=ref, send_sem=ag_send.at[a], recv_sem=ag_recv[a].at[c],
            device_id=peer(stages - 1 - a, c), device_id_type=MESH)

    def far_copy(o, c):
        ref = out.at[block(places, c), :, cols(c)]
        return pltpu.make_async_remote_copy(
            src_ref=ref, dst_ref=ref, send_sem=far_send, recv_sem=far_recv,
            device_id=(row, (col + o) % n_col), device_id_type=MESH)

    def total_of(ref, sem):
        return pltpu.make_async_copy(ref, ref, sem)

    def arrived(s, c):
        if s == 0:
            for copy in weights(c, c % BUFFERS):
                copy.wait()
        else:
            rs_copy(s - 1, c).wait_recv()

    def worked(s, c):
        if s == 0:
            x = xg[...].reshape(-1, xg.shape[-1])
            for k in range(2):
                part = jnp.dot(x, wbuf[c % BUFFERS, k], preferred_element_type=jnp.float32)
                acc[c, :, k] = part.reshape(n_col, -1, width)
            coded(0, acc, c)
            return
        i = s - 1
        source = acc if i == 0 else held[i - 1]
        if i < stages - 1:
            def keep(g, k, total):
                held[i][c, g, k] = total

            summed(i, source, c, keep)
            coded(s, held[i], c)
        else:
            sums = []
            summed(i, source, c, lambda g, k, total: sums.append(total))
            gate, up = sums
            hidden = (gate / (1.0 + jnp.exp(-gate)) * up).astype(jnp.bfloat16)
            out[block(places, c), :, cols(c)] = hidden

    def sent(s, c):
        if s < stages:
            rs_copy(s, c).start()
        if s == 0:
            @pl.when(c + BUFFERS < chunks)
            def _():
                for copy in weights(c + BUFFERS, c % BUFFERS):
                    copy.start()
        if s == stages:
            @pl.when(c < chunks - direct)
            def _():
                ag_copy(0, c, False).start()

            @pl.when(c >= chunks - direct)
            def _():
                for o in range(1, n_col):
                    far_copy(o, c).start()

    def passed(a, c):
        @pl.when(jnp.logical_and(c >= 0, c < chunks - direct))
        def _():
            ag_copy(a, c, True).wait_recv()
            if a < stages - 1:
                ag_copy(a + 1, c, False).start()

    lags = (list(LAGS) + [LAGS[-1] + 3 * (i + 1) for i in range(stages)])[: 1 + stages]
    ag_lags = [lags[-1] + GATHER_LAG * (a + 1) for a in range(stages)]
    bounds = sorted({0, *lags, *[lag + chunks for lag in lags], chunks + ag_lags[-1]})
    for first, last in zip(bounds, bounds[1:]):
        active = [s for s, lag in enumerate(lags) if lag <= first < lag + chunks]

        def turn(t, carry, active=active):
            for act in (arrived, worked, sent):
                for s in active[::-1]:
                    act(s, t - lags[s])
            for a, lag in enumerate(ag_lags):
                passed(a, t - lag)
            return carry

        lax.fori_loop(first, last, turn, 0)

    for i in range(stages):
        total_of(sends[i], rs_send.at[i]).wait()
    near = (chunks - direct) * width
    if near:
        for a in range(stages):
            total_of(out.at[pl.ds(0, 2**a), :, pl.ds(0, near)], ag_send.at[a]).wait()
    if direct:
        far = out.at[pl.ds(0, n_col - 1), :, pl.ds(near, direct * width)]
        total_of(far, far_send).wait()
        total_of(far, far_recv).wait()


def solution(mesh):
    n_row, n_col = mesh.shape["row"], mesh.shape["col"]

    def local(tokens, gate_weight, up_weight):
        own_tokens, depth = tokens.shape
        columns = gate_weight.shape[1]
        each = own_tokens * n_row // n_col
        width = max(w for w in range(128, WIDEST + 1, 128) if columns % w == 0)
        chunks = columns // width
        digits = digits_of(n_col)
        radices = tuple(radix for _, radix in digits)
        subs, count = [], n_col
        for radix in radices:
            count //= radix
            subs.append(count)
        parts = [(chunks, each, 2 * sub * width + LANES) for sub in subs]
        scratch = [
            pltpu.VMEM((n_row, own_tokens, depth), jnp.bfloat16),
            pltpu.VMEM((BUFFERS, 2, depth, width), jnp.bfloat16),
            pltpu.VMEM((chunks, n_col, 2, each, width), jnp.float32),
        ]
        scratch += [pltpu.VMEM((chunks, sub, 2, each, width), jnp.float32) for sub in subs[:-1]]
        scratch += [pltpu.VMEM(shape, jnp.bfloat16) for shape in parts]
        scratch += [pltpu.VMEM(shape, jnp.bfloat16) for shape in parts]
        dma = pltpu.SemaphoreType.DMA
        scratch += [dma, dma((n_row - 1,)), dma((n_row - 1,)), dma((BUFFERS, 2))]
        scratch += [dma, dma, dma((len(digits),)), dma((len(digits),))]
        scratch += [dma((chunks,))] * len(digits) + [dma((max(chunks - FAR, 1),))] * len(digits)
        out = pl.pallas_call(
            functools.partial(kernel, n_row, n_col, chunks, width),
            out_shape=pltpu.VMEM((n_col, each, columns), jnp.bfloat16),
            in_specs=[pl.BlockSpec(memory_space=pl.ANY)] * 3,
            out_specs=pl.BlockSpec(memory_space=pltpu.VMEM),
            scratch_shapes=scratch,
            compiler_params=pltpu.CompilerParams(
                collective_id=0, has_side_effects=True, vmem_limit_bytes=56 * 2**20),
        )(tokens, gate_weight, up_weight)
        return out.reshape(n_col * each, columns)

    in_specs = (P("row", "col"), P("col", "row"), P("col", "row"))
    return jax.shard_map(local, mesh=mesh, in_specs=in_specs, out_specs=P(None, "row"), check_vma=False)
```

time: 57.3 us -> 48.3 us (0.84)
  Pallas kernels: 55 us -> 47.3 us
  local copies, waits for them, and re-layouts: 2.11 us -> 0.9 us
    pallas_call x1, Pallas kernels: 55 us -> 47.3 us  [local(): pl.pallas_call(functools.partial(kernel, n_row, n_col, chunks, width), ou...]
    unnamed x1, local copies, waits for them, and re-layouts: 2.11 us -> 0.9 us
where the time goes in v1:
time: 48.3 us; the launch traced here: 48.2 us
  Pallas kernels  47.3 us (98%)
  local copies, waits for them, and re-layouts  0.9 us (2%)
    pallas_call x1, Pallas kernels, local(): pl.pallas_call(functools.partial(kernel, n_row, n_col, chunks, width), ou...  47.3 us

profile of v1, /device:TPU:0, one launch (start us, length us, event | category | flops | bytes accessed | tf_op | source)
XLA Modules:
  0.0 48.2 jit_solution(17105404190445463588)
XLA Ops:
  0.0 47.3 %shard_map.37 = bf16[8,8,6656]{2,1,0:T(8,128)(2,1)S(1)} custom-call(bf16[16,2048]{1,0:T(8,128)(2,1)} %tok_hbm.1, bf16[2048,6656]{1,0:T(8,128)(2,1)} %gate_hbm.1, bf16[2048,6656]{1,0:T(8,128)(2,1)} %up_hbm.1), custom_call_target="tpu_custom_call" | custom-call | tf_op jit(solution)/shard_map/pallas_call | solution.py:280
  47.3 0.9 %copy.5 = bf16[64,6656]{1,0:T(8,128)(2,1)} copy(bf16[64,6656]{1,0:T(8,128)(2,1)S(1)} %bitcast.1) | data formatting | bytes 1703936

commit v2 on v1

--- a/solution.py
+++ b/solution.py
@@ -10,9 +10,9 @@
 MESH = pl.DeviceIdType.MESH
 
 BUFFERS = 8
-LAGS = (0, 4, 7, 10)
+LAGS = (0, 4, 8, 12)
 GATHER_LAG = 3
-FAR = 4
+FAR = (4, 2)
 SWAP_EVERY = 4
 SWAP_AT = (1, 3)
 WIDEST = 512
@@ -44,7 +44,6 @@
 
 def kernel(n_row, n_col, chunks, width, tok_hbm, gate_hbm, up_hbm, out, *scratch):
     stages = len(digits_of(n_col))
-    direct = min(FAR, chunks)
     xg, wbuf, acc = scratch[0:3]
     held = scratch[3 : 2 + stages]
     scratch = scratch[2 + stages :]
@@ -55,11 +54,14 @@
     rs_recv, ag_recv = scratch[2 : 2 + stages], scratch[2 + stages :]
 
     row, col = lax.axis_index("row"), lax.axis_index("col")
+    side = row % 2
+    directs = [min(far, chunks) for far in FAR]
+    direct = jnp.where(side == 0, *directs)
 
     def weights(c, slot):
         cols = pl.ds(pl.multiple_of(c * width, width), width)
         return [
-            pltpu.make_async_copy(hbm.at[:, cols], wbuf.at[slot, k], w_sem.at[slot, k])
+            pltpu.make_async_copy(hbm.at[:, cols], wbuf.at[slot, k], w_sem.at[slot])
             for k, hbm in enumerate((gate_hbm, up_hbm))
         ]
 
@@ -80,17 +82,16 @@
             copy.start()
     pl.semaphore_wait(barrier, greeted)
 
-    def token_copy(o, place):
-        return pltpu.make_async_remote_copy(
-            src_ref=xg.at[place], dst_ref=xg.at[place], send_sem=tok_send.at[o - 1], recv_sem=tok_recv.at[o - 1],
-            device_id=((row + o) % n_row, col), device_id_type=MESH)
+    def total_of(ref, sem):
+        return pltpu.make_async_copy(ref, ref, sem)
 
     for o in range(1, n_row):
-        token_copy(o, row).start()
-    for o in range(1, n_row):
-        token_copy(o, (row + n_row - o) % n_row).wait_recv()
-    for o in range(1, n_row):
-        token_copy(o, row).wait_send()
+        pltpu.make_async_remote_copy(
+            src_ref=xg.at[row], dst_ref=xg.at[row], send_sem=tok_send, recv_sem=tok_recv,
+            device_id=((row + o) % n_row, col), device_id_type=MESH).start()
+    others = xg.at[pl.ds(0, n_row - 1)]
+    total_of(others, tok_recv).wait()
+    total_of(others, tok_send).wait()
 
     low = lax.broadcasted_iota(jnp.int32, (xg.shape[0] * xg.shape[1] // n_col, LANES), 1) < LANES // 2
 
@@ -154,7 +155,7 @@
         start = (own + (1 - 2 * (own % 2)) if back else own) * 2**a
         ref = out.at[pl.ds(start, 2**a), :, cols(c)]
         return pltpu.make_async_remote_copy(
-            src_ref=ref, dst_ref=ref, send_sem=ag_send.at[a], recv_sem=ag_recv[a].at[c],
+            src_ref=ref, dst_ref=ref, send_sem=ag_send.at[a], recv_sem=ag_recv[a].at[c if a < stages - 1 else 0],
             device_id=peer(stages - 1 - a, c), device_id_type=MESH)
 
     def far_copy(o, c):
@@ -163,13 +164,9 @@
             src_ref=ref, dst_ref=ref, send_sem=far_send, recv_sem=far_recv,
             device_id=(row, (col + o) % n_col), device_id_type=MESH)
 
-    def total_of(ref, sem):
-        return pltpu.make_async_copy(ref, ref, sem)
-
     def arrived(s, c):
         if s == 0:
-            for copy in weights(c, c % BUFFERS):
-                copy.wait()
+            total_of(wbuf.at[c % BUFFERS], w_sem.at[c % BUFFERS]).wait()
         else:
             rs_copy(s - 1, c).wait_recv()
 
@@ -218,11 +215,10 @@
         @pl.when(jnp.logical_and(c >= 0, c < chunks - direct))
         def _():
             ag_copy(a, c, True).wait_recv()
-            if a < stages - 1:
-                ag_copy(a + 1, c, False).start()
+            ag_copy(a + 1, c, False).start()
 
     lags = (list(LAGS) + [LAGS[-1] + 3 * (i + 1) for i in range(stages)])[: 1 + stages]
-    ag_lags = [lags[-1] + GATHER_LAG * (a + 1) for a in range(stages)]
+    ag_lags = [lags[-1] + GATHER_LAG * (a + 1) for a in range(stages - 1)]
     bounds = sorted({0, *lags, *[lag + chunks for lag in lags], chunks + ag_lags[-1]})
     for first, last in zip(bounds, bounds[1:]):
         active = [s for s, lag in enumerate(lags) if lag <= first < lag + chunks]
@@ -239,14 +235,18 @@
 
     for i in range(stages):
         total_of(sends[i], rs_send.at[i]).wait()
-    near = (chunks - direct) * width
-    if near:
-        for a in range(stages):
-            total_of(out.at[pl.ds(0, 2**a), :, pl.ds(0, near)], ag_send.at[a]).wait()
-    if direct:
-        far = out.at[pl.ds(0, n_col - 1), :, pl.ds(near, direct * width)]
-        total_of(far, far_send).wait()
-        total_of(far, far_recv).wait()
+    for which, far in enumerate(directs):
+        @pl.when(side == which)
+        def _(far=far):
+            near = (chunks - far) * width
+            if near:
+                for a in range(stages):
+                    total_of(out.at[pl.ds(0, 2**a), :, pl.ds(0, near)], ag_send.at[a]).wait()
+                total_of(out.at[pl.ds(0, n_col // 2), :, pl.ds(0, near)], ag_recv[-1].at[0]).wait()
+            if far:
+                ref = out.at[pl.ds(0, n_col - 1), :, pl.ds(near, far * width)]
+                total_of(ref, far_send).wait()
+                total_of(ref, far_recv).wait()
 
 
 def solution(mesh):
@@ -274,9 +274,9 @@
         scratch += [pltpu.VMEM(shape, jnp.bfloat16) for shape in parts]
         scratch += [pltpu.VMEM(shape, jnp.bfloat16) for shape in parts]
         dma = pltpu.SemaphoreType.DMA
-        scratch += [dma, dma((n_row - 1,)), dma((n_row - 1,)), dma((BUFFERS, 2))]
+        scratch += [dma, dma, dma, dma((BUFFERS,))]
         scratch += [dma, dma, dma((len(digits),)), dma((len(digits),))]
-        scratch += [dma((chunks,))] * len(digits) + [dma((max(chunks - FAR, 1),))] * len(digits)
+        scratch += [dma((chunks,))] * len(digits) + [dma((max(chunks - min(FAR), 1),))] * (len(digits) - 1) + [dma((1,))]
         out = pl.pallas_call(
             functools.partial(kernel, n_row, n_col, chunks, width),
             out_shape=pltpu.VMEM((n_col, each, columns), jnp.bfloat16),

time: 48.3 us -> 46.7 us (0.967)
  Pallas kernels: 47.3 us -> 45.6 us
    pallas_call x1, Pallas kernels: 47.3 us -> 45.6 us  [local(): pl.pallas_call(functools.partial(kernel, n_row, n_col, chunks, width), ou...]
where the time goes in v2:
time: 46.7 us; the launch traced here: 46.5 us
  Pallas kernels  45.6 us (98%)
  local copies, waits for them, and re-layouts  0.9 us (2%)
    pallas_call x1, Pallas kernels, local(): pl.pallas_call(functools.partial(kernel, n_row, n_col, chunks, width), ou...  45.6 us

profile of v2, /device:TPU:0, one launch (start us, length us, event | category | flops | bytes accessed | tf_op | source)
XLA Modules:
  0.0 46.5 jit_solution(12648655561315618411)
XLA Ops:
  0.0 45.6 %shard_map.37 = bf16[8,8,6656]{2,1,0:T(8,128)(2,1)S(1)} custom-call(bf16[16,2048]{1,0:T(8,128)(2,1)} %tok_hbm.1, bf16[2048,6656]{1,0:T(8,128)(2,1)} %gate_hbm.1, bf16[2048,6656]{1,0:T(8,128)(2,1)} %up_hbm.1), custom_call_target="tpu_custom_call" | custom-call | tf_op jit(solution)/shard_map/pallas_call | solution.py:280
  45.6 0.9 %copy.5 = bf16[64,6656]{1,0:T(8,128)(2,1)} copy(bf16[64,6656]{1,0:T(8,128)(2,1)S(1)} %bitcast.1) | data formatting | bytes 1703936

commit v3 on v2

--- a/solution.py
+++ b/solution.py
@@ -208,7 +208,7 @@
 
             @pl.when(c >= chunks - direct)
             def _():
-                for o in range(1, n_col):
+                for o in range(1, n_col)[::-1]:
                     far_copy(o, c).start()
 
     def passed(a, c):

time: 46.7 us -> 46.5 us (level)
  no operation moved by 1% of the time
where the time goes in v3:
time: 46.5 us; the launch traced here: 46.4 us
  Pallas kernels  45.5 us (98%)
  local copies, waits for them, and re-layouts  0.9 us (2%)
    pallas_call x1, Pallas kernels, local(): pl.pallas_call(functools.partial(kernel, n_row, n_col, chunks, width), ou...  45.5 us

profile of v3, /device:TPU:0, one launch (start us, length us, event | category | flops | bytes accessed | tf_op | source)
XLA Modules:
  0.0 46.4 jit_solution(8623408383288295195)
XLA Ops:
  0.0 45.5 %shard_map.37 = bf16[8,8,6656]{2,1,0:T(8,128)(2,1)S(1)} custom-call(bf16[16,2048]{1,0:T(8,128)(2,1)} %tok_hbm.1, bf16[2048,6656]{1,0:T(8,128)(2,1)} %gate_hbm.1, bf16[2048,6656]{1,0:T(8,128)(2,1)} %up_hbm.1), custom_call_target="tpu_custom_call" | custom-call | tf_op jit(solution)/shard_map/pallas_call | solution.py:280
  45.5 0.9 %copy.5 = bf16[64,6656]{1,0:T(8,128)(2,1)} copy(bf16[64,6656]{1,0:T(8,128)(2,1)S(1)} %bitcast.1) | data formatting | bytes 1703936
